TPU v7x, 32 devices: a whole 2x2x4 slice. The times are simulated.
32 devices in a mesh: col: 8 (over y, x, core), row: 4 (over z).
Axes of the slice: x: 2, y: 2, z: 4, core: 2. Of those that a mesh axis runs over, the one named last changes fastest.
Arguments:
- rhs: float32 [2, 32, 4, 4096], P(None, None, 'row', 'col'), may hold values from -6 to 6
- u_factor: bfloat16 [64, 40, 2, 256, 128], P('row', 'col'), may hold values from -0.078125 to 0.078125
- v_factor: bfloat16 [64, 40, 2, 256, 128], P('row', 'col'), may hold values from -0.375 to 0.375
- ranks: int32 [64, 40], P('row', 'col'), may hold values from 8 to 128, as said below
- assign: int32 [40], replicated, may hold values from 0 to 39, each once
Outputs:
- solution: float32 [2, 32, 10240], P(None, None, 'col')
- residual_estimate: float32 [32], replicated
Inputs may be any that keep to these rules, and one draw needn't show every extreme that they name: `ranks`: every entry is 128 // 16 times a power of two from 1 to 16.
All inputs are finite; a program needn't handle non-finite values.
Results may differ from a plain program's by a relative error of at most 0.0068.
Values may be sent and summed in bfloat16 or wider, within the bound.
No kernel may reach another device: no remote copies, remote signals or barrier semaphores. Data moves between devices by JAX's collectives and lax.ppermute only.
A program may use at most 128 MiB of HBM per device.

v0:
```python
import jax
import jax.numpy as jnp
from jax import lax
from jax.sharding import PartitionSpec as P

ITERS = 2


def sum_squares(value):
    return jnp.sum(value * value, axis=(0, 2))


def on_device(rhs, u_factor, v_factor, ranks, assign):
    tile_rows = u_factor.shape[0]
    tile_cols = u_factor.shape[1]
    tile_size = u_factor.shape[3]
    rank_cap = u_factor.shape[4]
    sources = rhs.shape[1]
    rank_iota = lax.broadcasted_iota(jnp.int32, (tile_rows, tile_cols, 1, 1, rank_cap), 4)
    mask = (rank_iota < ranks[:, :, None, None, None]).astype(jnp.float32)

    def adjoint_terms(group_data):
        data_b = group_data.reshape(2, sources, tile_rows, tile_size)
        raw = jnp.einsum("ipcnk,dsin->ipcdsk", u_factor, data_b, preferred_element_type=jnp.float32)
        coeff = jnp.stack(
            [raw[:, :, 0, 0] + raw[:, :, 1, 1], raw[:, :, 0, 1] - raw[:, :, 1, 0]], axis=2
        )
        coeff = (coeff * mask).astype(jnp.bfloat16)
        prod = jnp.einsum("ipcnk,ipdsk->cdspn", v_factor, coeff, preferred_element_type=jnp.float32)
        partial_model = jnp.stack([prod[0, 0] + prod[1, 1], prod[0, 1] - prod[1, 0]], axis=0)
        return partial_model.reshape(2, sources, tile_cols * tile_size)

    def adjoint_step(data_hat, v_prev):
        group_data = lax.all_gather(data_hat.astype(jnp.bfloat16), "col", axis=2, tiled=True)
        beta_now = jnp.sqrt(lax.psum(sum_squares(data_hat), ("col", "row")))
        model_sum = lax.psum(adjoint_terms(group_data), "row")
        v_hat = model_sum / beta_now[None, :, None] - beta_now[None, :, None] * v_prev
        alpha_now = jnp.sqrt(lax.psum(sum_squares(v_hat), "col"))
        return (
            data_hat / beta_now[None, :, None],
            beta_now,
            v_hat / alpha_now[None, :, None],
            alpha_now,
        )

    data_first = rhs.reshape(2, sources, rhs.shape[3])
    zero_model = jnp.zeros((2, sources, tile_cols * tile_size), jnp.float32)
    u_vec, beta_now, v_vec, alpha_now = adjoint_step(data_first, zero_model)
    w_vec = v_vec
    x_vec = zero_model
    phibar = beta_now
    rhobar = alpha_now
    for iteration in range(ITERS):
        model_b = v_vec.astype(jnp.bfloat16).reshape(2, sources, tile_cols, tile_size)
        forward_raw = jnp.einsum(
            "ipcnk,dspn->ipcdsk", v_factor, model_b, preferred_element_type=jnp.float32
        )
        forward_coeff = jnp.stack(
            [
                forward_raw[:, :, 0, 0] - forward_raw[:, :, 1, 1],
                forward_raw[:, :, 0, 1] + forward_raw[:, :, 1, 0],
            ],
            axis=2,
        )
        forward_coeff = (forward_coeff * mask).astype(jnp.bfloat16)
        forward_prod = jnp.einsum(
            "ipcnk,ipdsk->cdsin", u_factor, forward_coeff, preferred_element_type=jnp.float32
        )
        partial_data = jnp.stack(
            [forward_prod[0, 0] - forward_prod[1, 1], forward_prod[0, 1] + forward_prod[1, 0]],
            axis=0,
        )
        partial_data = partial_data.reshape(2, sources, tile_rows * tile_size)
        data_hat = (
            lax.psum_scatter(partial_data, "col", scatter_dimension=2, tiled=True)
            - alpha_now[None, :, None] * u_vec
        )
        u_vec, beta_now, v_vec, alpha_now = adjoint_step(data_hat, v_vec)
        rho_now = jnp.sqrt(rhobar * rhobar + beta_now * beta_now)
        cosine = rhobar / rho_now
        sine = beta_now / rho_now
        theta = sine * alpha_now
        rhobar = -cosine * alpha_now
        phi_now = cosine * phibar
        phibar = sine * phibar
        x_vec = x_vec + (phi_now / rho_now)[None, :, None] * w_vec
        w_vec = v_vec - (theta / rho_now)[None, :, None] * w_vec
    all_cols = assign.shape[0]
    natural = lax.axis_index("col") * tile_cols + jnp.arange(tile_cols, dtype=jnp.int32)
    positions = jnp.arange(all_cols, dtype=jnp.int32)
    where_held = jnp.sum(
        positions[None, :] * (assign[None, :] == natural[:, None]).astype(jnp.int32), axis=1
    )
    share = sources // lax.axis_size("row")
    own_share = lax.dynamic_slice_in_dim(x_vec, lax.axis_index("row") * share, share, 1)
    gathered = lax.all_gather(own_share, "col", axis=2, tiled=True)
    gathered = gathered.reshape(2, share, all_cols, tile_size)
    picked = jnp.take(gathered, where_held, axis=2).reshape(2, share, tile_cols * tile_size)
    solution = lax.all_gather(picked, "row", axis=1, tiled=True)
    return (solution, phibar)


def solution(mesh):
    in_specs = (
        P(None, None, "row", "col"),
        P("row", "col", None, None, None),
        P("row", "col", None, None, None),
        P("row", "col"),
        P(),
    )
    out_specs = (P(None, None, "col"), P())
    return jax.shard_map(
        on_device, mesh=mesh, in_specs=in_specs, out_specs=out_specs, check_vma=False
    )
```

profile of v0, /device:TPU:0, one launch (start us, length us, event | category | flops | bytes accessed | tf_op | source)
XLA Modules:
  0.0 338.9 jit_solution(15961958501180942365)
XLA Ops:
  7.2 0.9 copy.217
  8.1 11.3 %all_gather.12 = bf16[2,32,4096]{2,1,0:T(8,128)(2,1)S(1)} all-gather(bf16[2,32,512]{2,1,0:T(8,128)(2,1)S(1)} %bitcast.164), channel_id=1, replica_groups=mesh['col'=8,'row'=4] {'col'}, dimensions={2}, use_global_device_ids=true | all-gather | bytes 589824 | tf_op jit(solution)/shard_map/all_gather | solution.py:34
  19.6 6.1 %fusion.29 = f32[16,5,2,2,32,128]{5,4,2,1,3,0:T(8,128)S(1)} fusion(bf16[16,5,2,256,128]{4,3,2,1,0:T(8,128)(2,1)} %param.6, bf16[2,32,16,256,1,1]{3,2,1,0,5,4:T(8,128)(2,1)S(1)} %bitcast_bitcast_fusion.1), kind=kOutput, calls=%fused_computation.28 | convolution fusion | flops 671088640 | bytes 16252928 | tf_op jit(solution)/shard_map/ipcnk,dsin->ipcdsk/dot_general | solution.py:24
  25.7 0.3 fusion.48
  26.0 0.3 fusion.50
  26.3 0.4 copy-done.1
  26.8 5.9 %fusion.55 = f32[2,2,32,5,256]{4,2,0,1,3:T(8,128)S(1)} fusion(bf16[16,5,2,256,128]{4,3,2,1,0:T(8,128)(2,1)} %param.7, f32[16,5,1,32,128]{4,3,1,0,2:T(8,128)S(1)} %fusion.48, f32[16,5,1,32,128]{4,3,1,0,2:T(8,128)S(1)} %fusion.50, f32[16,5,128]{2,1,0:T(8,128)S(1)} %fusion.74), kind=kOutput, calls=%fused_computation.57 | convolution fusion | flops 673054720 | bytes 13803520 | tf_op jit(solution)/shard_map/ipcnk,ipdsk->cdspn/dot_general | solution.py:29
  33.2 0.7 pad_maximum_fusion.2
  34.1 39.7 %psum.50 = f32[32]{0:T(128)S(1)} all-reduce(f32[32]{0:T(128)S(1)} %fusion.69), channel_id=1, replica_groups=mesh['col'=8,'row'=4] {'col','row'}, use_global_device_ids=true, to_apply=%region_3.0 | all-reduce | flops 32 | bytes 256 | tf_op jit(solution)/shard_map/psum | solution.py:35
  73.9 1.2 multiply_reduce_fusion.1
  75.1 12.7 %psum.51 = f32[32]{0:T(128)S(1)} all-reduce(f32[32]{0:T(128)S(1)} %multiply_reduce_fusion.1), channel_id=1, replica_groups=mesh['col'=8,'row'=4] {'col'}, use_global_device_ids=true, to_apply=%region_5.0 | all-reduce | flops 32 | bytes 256 | tf_op jit(solution)/shard_map/psum | solution.py:38
  87.8 1.2 fusion.78
  89.0 0.2 reshape.383
  89.2 5.2 %fusion.20 = f32[16,5,2,2,32,128]{5,4,1,0,3,2:T(8,128)S(1)} fusion(bf16[2,32,5,256,1,1]{3,2,1,0,5,4:T(8,128)(2,1)S(1)} %bitcast.160, bf16[16,5,2,256,128]{4,3,2,1,0:T(8,128)(2,1)} %param.7), kind=kOutput, calls=%fused_computation.25 | convolution fusion | flops 671088640 | bytes 15892480 | tf_op jit(solution)/shard_map/ipcnk,dspn->ipcdsk/dot_general | solution.py:55
  94.5 1.7 fusion.47
  96.2 4.6 %fusion.32 = f32[2,2,32,16,256]{4,2,0,1,3:T(8,128)S(1)} fusion(bf16[16,5,2,256,128]{4,3,2,1,0:T(8,128)(2,1)S(1)} %bitcast.150, f32[16,5,1,32,128]{4,3,1,0,2:T(8,128)} %get-tuple-element.17, f32[16,5,1,32,128]{4,3,1,0,2:T(8,128)S(1)} %get-tuple-element.16, f32[16,5,128]{2,1,0:T(8,128)S(1)} %fusion.74), kind=kOutput, calls=%fused_computation.29 | convolution fusion | flops 673054720 | bytes 15245312 | tf_op jit(solution)/shard_map/ipcnk,ipdsk->cdsin/dot_general | solution.py:66
  100.9 0.3 copy.94
  101.4 0.3 copy.93
  101.8 1.0 pad_maximum_fusion
  102.9 35.1 %reduce-scatter.3.cloned.1.call-done = f32[2,32,512]{2,1,0:T(8,128)} async-done(((f32[2,32,4096]{2,1,0:T(8,128)}), f32[2,32,512]{2,1,0:T(8,128)}) %reduce-scatter.3.cloned.1.call-update) | async-done | bytes 131088 | tf_op jit(solution)/shard_map/reduce_scatter | solution.py:75
  138.0 1.1 multiply_reduce_fusion.3
  139.1 10.0 %all_gather.13 = bf16[2,32,4096]{2,1,0:T(8,128)(2,1)S(1)} all-gather(bf16[2,32,512]{2,1,0:T(8,128)(2,1)S(1)} %convert_element_type.38), channel_id=1, replica_groups=mesh['col'=8,'row'=4] {'col'}, dimensions={2}, use_global_device_ids=true | all-gather | bytes 589824 | tf_op jit(solution)/shard_map/all_gather | solution.py:34
  149.3 5.2 %fusion.26 = f32[16,5,2,2,32,128]{5,4,1,0,3,2:T(8,128)S(1)} fusion(bf16[2,32,16,256,1,1]{3,2,1,0,5,4:T(8,128)(2,1)S(1)} %bitcast_bitcast_fusion, bf16[16,5,2,256,128]{4,3,2,1,0:T(8,128)(2,1)} %param.6), kind=kOutput, calls=%fused_computation.27 | convolution fusion | flops 671088640 | bytes 16252928 | tf_op jit(solution)/shard_map/ipcnk,dsin->ipcdsk/dot_general | solution.py:24
  154.5 0.6 fusion.45
  155.1 0.5 slice-done.7
  155.7 0.6 slice-done.8
  156.3 3.3 fusion.60
  159.9 0.7 pad_maximum_fusion.3
  160.8 39.6 %psum.52 = f32[32]{0:T(128)S(1)} all-reduce(f32[32]{0:T(128)S(1)} %get-tuple-element.8), channel_id=1, replica_groups=mesh['col'=8,'row'=4] {'col','row'}, use_global_device_ids=true, to_apply=%region_8.0 | all-reduce | flops 32 | bytes 256 | tf_op jit(solution)/shard_map/psum | solution.py:35
  200.4 1.4 multiply_reduce_fusion
  201.7 12.7 %psum.54 = f32[32]{0:T(128)S(1)} all-reduce(f32[32]{0:T(128)S(1)} %multiply_reduce_fusion), channel_id=1, replica_groups=mesh['col'=8,'row'=4] {'col'}, use_global_device_ids=true, to_apply=%region_11.0 | all-reduce | flops 32 | bytes 256 | tf_op jit(solution)/shard_map/psum | solution.py:38
  214.4 1.1 fusion.76
  215.5 0.2 reshape.385
  215.8 5.2 %fusion.23 = f32[16,5,2,2,32,128]{5,4,1,0,3,2:T(8,128)S(1)} fusion(bf16[2,32,5,256,1,1]{3,2,1,0,5,4:T(8,128)(2,1)S(1)} %bitcast.161, bf16[16,5,2,256,128]{4,3,2,1,0:T(8,128)(2,1)} %param.7), kind=kOutput, calls=%fused_computation.26 | convolution fusion | flops 671088640 | bytes 15892480 | tf_op jit(solution)/shard_map/ipcnk,dspn->ipcdsk/dot_general | solution.py:55
  221.0 1.7 fusion.43
  222.7 4.6 %fusion.35 = f32[2,2,32,16,256]{4,2,0,1,3:T(8,128)S(1)} fusion(bf16[16,5,2,256,128]{4,3,2,1,0:T(8,128)(2,1)S(1)} %bitcast.152, f32[16,5,1,32,128]{4,3,1,0,2:T(8,128)} %get-tuple-element.13, f32[16,5,1,32,128]{4,3,1,0,2:T(8,128)S(1)} %get-tuple-element.12, f32[16,5,128]{2,1,0:T(8,128)S(1)} %fusion.74), kind=kOutput, calls=%fused_computation.30 | convolution fusion | flops 673054720 | bytes 15245312 | tf_op jit(solution)/shard_map/ipcnk,ipdsk->cdsin/dot_general | solution.py:66
  227.4 0.3 copy.107
  227.9 0.3 copy.106
  228.3 1.0 pad_maximum_fusion.1
  229.4 0.2 select_reduce_fusion
  229.7 34.9 %reduce-scatter.5.cloned.1.call-done = f32[2,32,512]{2,1,0:T(8,128)} async-done(((f32[2,32,4096]{2,1,0:T(8,128)}), f32[2,32,512]{2,1,0:T(8,128)}) %reduce-scatter.5.cloned.1.call-update) | async-done | bytes 131088 | tf_op jit(solution)/shard_map/reduce_scatter | solution.py:75
  264.6 1.1 multiply_reduce_fusion.2
  265.7 39.3 %psum.55 = f32[32]{0:T(128)S(1)} all-reduce(f32[32]{0:T(128)S(1)} %multiply_reduce_fusion.2), channel_id=1, replica_groups=mesh['col'=8,'row'=4] {'col','row'}, use_global_device_ids=true, to_apply=%region_14.0 | all-reduce | flops 32 | bytes 256 | tf_op jit(solution)/shard_map/psum | solution.py:35
  305.0 0.6 divide_multiply_fusion
  305.9 10.9 %all_gather.14 = f32[2,8,10240]{2,1,0:T(8,128)S(1)} all-gather(f32[2,8,1280]{2,1,0:T(8,128)S(1)} %fusion.73), channel_id=1, replica_groups=mesh['col'=8,'row'=4] {'col'}, dimensions={2}, use_global_device_ids=true | all-gather | bytes 737280 | tf_op jit(solution)/shard_map/all_gather | solution.py:96
  316.8 0.5 gather_fusion
  317.4 14.3 %all_gather.15 = f32[2,32,1280]{2,1,0:T(8,128)S(1)} all-gather(f32[2,8,1280]{2,1,0:T(8,128)S(1)} %broadcast_select_fusion), channel_id=1, replica_groups=mesh['col'=8,'row'=4] {'row'}, dimensions={1}, use_global_device_ids=true | all-gather | bytes 409600 | tf_op jit(solution)/shard_map/all_gather | solution.py:99
  331.7 0.7 copy.221
  (75 shorter events, 2.8 us)
Async XLA Ops:
  7.2 66.7 %all-reduce.3.cloned.1.call-start = ((), (), s32[]{:S(2)}) async-start(), calls=%async_computation.2 | async-start | bytes 655360 | tf_op jit(solution)/shard_map/psum | solution.py:36
  26.0 0.7 copy-start.1
  32.7 1.3 copy-start
  33.9 104.1 %reduce-scatter.3.cloned.1.call-start = ((), (), s32[]{:S(2)}) async-start(), calls=%async_computation.3 | async-start | bytes 1179648 | tf_op jit(solution)/shard_map/reduce_scatter | solution.py:75
  87.8 8.4 %slice-start = ((s8[10485760]{0:T(1024)(128)(4,1)}), s8[2097152]{0:T(1024)(128)(4,1)S(1)}, s32[]{:S(2)}) async-start(s8[10485760]{0:T(1024)(128)(4,1)} %bitcast.149), calls=%async_computation.6 | async-start | bytes 4194304
  89.2 6.9 %slice-start.1 = ((s8[10485760]{0:T(1024)(128)(4,1)}), s8[4194304]{0:T(1024)(128)(4,1)S(1)}, s32[]{:S(2)}) async-start(s8[10485760]{0:T(1024)(128)(4,1)} %bitcast.149), calls=%async_computation.7 | async-start | bytes 8388608
  89.2 6.9 %slice-start.2 = ((s8[10485760]{0:T(1024)(128)(4,1)}), s8[4194304]{0:T(1024)(128)(4,1)S(1)}, s32[]{:S(2)}) async-start(s8[10485760]{0:T(1024)(128)(4,1)} %bitcast.149), calls=%async_computation.8 | async-start | bytes 8388608
  102.8 97.5 %all-reduce.5.cloned.1.call-start = ((), (), s32[]{:S(2)}) async-start(), calls=%async_computation.4 | async-start | bytes 655360 | tf_op jit(solution)/shard_map/psum | solution.py:36
  149.1 6.0 %slice-start.6 = ((s8[10485760]{0:T(1024)(128)(4,1)}), s8[4194304]{0:T(1024)(128)(4,1)S(1)}, s32[]{:S(2)}) async-start(s8[10485760]{0:T(1024)(128)(4,1)} %bitcast.153), calls=%async_computation.12 | async-start | bytes 8388608
  149.3 6.4 %slice-start.7 = ((s8[10485760]{0:T(1024)(128)(4,1)}), s8[4194304]{0:T(1024)(128)(4,1)S(1)}, s32[]{:S(2)}) async-start(s8[10485760]{0:T(1024)(128)(4,1)} %bitcast.153), calls=%async_computation.13 | async-start | bytes 8388608
  149.3 7.0 %slice-start.8 = ((s8[10485760]{0:T(1024)(128)(4,1)}), s8[2097152]{0:T(1024)(128)(4,1)S(1)}, s32[]{:S(2)}) async-start(s8[10485760]{0:T(1024)(128)(4,1)} %bitcast.153), calls=%async_computation.14 | async-start | bytes 4194304
  160.7 103.9 %reduce-scatter.5.cloned.1.call-start = ((), (), s32[]{:S(2)}) async-start(), calls=%async_computation.5 | async-start | bytes 1179648 | tf_op jit(solution)/shard_map/reduce_scatter | solution.py:75
  200.4 22.3 %slice-start.3 = ((s8[10485760]{0:T(1024)(128)(4,1)}), s8[2097152]{0:T(1024)(128)(4,1)S(1)}, s32[]{:S(2)}) async-start(s8[10485760]{0:T(1024)(128)(4,1)} %bitcast.151), calls=%async_computation.9 | async-start | bytes 4194304
  215.7 6.9 %slice-start.4 = ((s8[10485760]{0:T(1024)(128)(4,1)}), s8[4194304]{0:T(1024)(128)(4,1)S(1)}, s32[]{:S(2)}) async-start(s8[10485760]{0:T(1024)(128)(4,1)} %bitcast.151), calls=%async_computation.10 | async-start | bytes 8388608
  215.7 6.9 %slice-start.5 = ((s8[10485760]{0:T(1024)(128)(4,1)}), s8[4194304]{0:T(1024)(128)(4,1)S(1)}, s32[]{:S(2)}) async-start(s8[10485760]{0:T(1024)(128)(4,1)} %bitcast.151), calls=%async_computation.11 | async-start | bytes 8388608
  227.9 1.5 copy-start.2
Sparse Core Ops, SparseCore 0:
  34.0 36.6 all-reduce.2
  103.0 34.9 reduce-scatter.2
  160.8 36.2 all-reduce.4
  229.5 35.0 reduce-scatter.4
where the time goes:
time: 340 us; the launch traced here: 339 us
  blocking collectives  190 us (56%)
  waiting for transfers between devices  70.1 us (21%)
  matrix products  40 us (12%)
  other arithmetic  16.8 us (5%)
  between operations  14.3 us (4%)
  local copies, waits for them, and re-layouts  7.14 us (2%)
    psum x3, blocking collectives, adjoint_step(): beta_now = jnp.sqrt(lax.psum(sum_squares(data_hat), ('col', 'row')))  119 us
    reduce_scatter x2, waiting for transfers between devices, on_device(): lax.psum_scatter(partial_data, 'col', scatter_dimension=2, tiled=True)  70 us
    psum x2, blocking collectives, adjoint_step(): alpha_now = jnp.sqrt(lax.psum(sum_squares(v_hat), 'col'))  25.4 us
    all_gather x2, blocking collectives, adjoint_step(): lax.all_gather(data_hat.astype(jnp.bfloat16), 'col', axis=2, tiled=True)  21.3 us
    all_gather x1, blocking collectives, on_device(): solution = lax.all_gather(picked, 'row', axis=1, tiled=True)  14.3 us
    dot_general x2, matrix products, adjoint_terms(): jnp.einsum('ipcnk,dsin->ipcdsk', u_factor, data_b, preferred_element_type...  11.3 us
    all_gather x1, blocking collectives, on_device(): gathered = lax.all_gather(own_share, 'col', axis=2, tiled=True)  10.9 us
    dot_general x2, matrix products, on_device(): jnp.einsum('ipcnk,dspn->ipcdsk', v_factor, model_b, preferred_element_typ...  10.4 us
  transfers between devices with their start and end apart: 4, of which 2 were waited for; matrix products, arithmetic and copies ran while one was open for 0% of the time, Pallas kernels for 0%

commit v1 on v0

--- a/solution.py
+++ b/solution.py
@@ -32,7 +32,7 @@
 
     def adjoint_step(data_hat, v_prev):
         group_data = lax.all_gather(data_hat.astype(jnp.bfloat16), "col", axis=2, tiled=True)
-        beta_now = jnp.sqrt(lax.psum(sum_squares(data_hat), ("col", "row")))
+        beta_now = jnp.sqrt(lax.psum(lax.psum(sum_squares(data_hat), "row"), "col"))
         model_sum = lax.psum(adjoint_terms(group_data), "row")
         v_hat = model_sum / beta_now[None, :, None] - beta_now[None, :, None] * v_prev
         alpha_now = jnp.sqrt(lax.psum(sum_squares(v_hat), "col"))

time: 340 us -> 315 us (0.926)
  blocking collectives: 190 us -> 141 us
  waiting for transfers between devices: 70.1 us -> 95.3 us
    psum x3 -> x6, blocking collectives: 119 us -> 70.9 us  [adjoint_step(): beta_now = jnp.sqrt(lax.psum(lax.psum(sum_squares(data_hat), 'row'), 'col'))]
    psum x2, waiting for transfers between devices: 0.01 us -> 25.6 us  [adjoint_step(): model_sum = lax.psum(adjoint_terms(group_data), 'row')]
  transfers between devices with their start and end apart: 4 -> 4, of which waited for: 2 -> 4; matrix products, arithmetic and copies ran while one was open for 0% -> 0% of each run, Pallas kernels for 0% -> 0%
where the time goes in v1:
time: 315 us; the launch traced here: 314 us
  blocking collectives  141 us (45%)
  waiting for transfers between devices  95.3 us (30%)
  matrix products  40 us (13%)
  other arithmetic  16.9 us (5%)
  between operations  14.2 us (5%)
  local copies, waits for them, and re-layouts  7.14 us (2%)
    psum x6, blocking collectives, adjoint_step(): beta_now = jnp.sqrt(lax.psum(lax.psum(sum_squares(data_hat), 'row'), 'col'))  70.9 us
    reduce_scatter x2, waiting for transfers between devices, on_device(): lax.psum_scatter(partial_data, 'col', scatter_dimension=2, tiled=True)  69.6 us
    psum x2, waiting for transfers between devices, adjoint_step(): model_sum = lax.psum(adjoint_terms(group_data), 'row')  25.6 us
    psum x2, blocking collectives, adjoint_step(): alpha_now = jnp.sqrt(lax.psum(sum_squares(v_hat), 'col'))  23.7 us
    all_gather x2, blocking collectives, adjoint_step(): lax.all_gather(data_hat.astype(jnp.bfloat16), 'col', axis=2, tiled=True)  21.3 us
    all_gather x1, blocking collectives, on_device(): solution = lax.all_gather(picked, 'row', axis=1, tiled=True)  14.8 us
    dot_general x2, matrix products, adjoint_terms(): jnp.einsum('ipcnk,dsin->ipcdsk', u_factor, data_b, preferred_element_type...  11.3 us
    dot_general x2, matrix products, on_device(): jnp.einsum('ipcnk,dspn->ipcdsk', v_factor, model_b, preferred_element_typ...  10.4 us
  transfers between devices with their start and end apart: 4, of which 4 were waited for; matrix products, arithmetic and copies ran while one was open for 0% of the time, Pallas kernels for 0%

profile of v1, /device:TPU:0, one launch (start us, length us, event | category | flops | bytes accessed | tf_op | source)
XLA Modules:
  0.0 314.5 jit_solution(141301255224520776)
XLA Ops:
  7.2 0.9 copy.217
  8.1 11.3 %all_gather.12 = bf16[2,32,4096]{2,1,0:T(8,128)(2,1)S(1)} all-gather(bf16[2,32,512]{2,1,0:T(8,128)(2,1)S(1)} %bitcast.164), channel_id=1, replica_groups=mesh['col'=8,'row'=4] {'col'}, dimensions={2}, use_global_device_ids=true | all-gather | bytes 589824 | tf_op jit(solution)/shard_map/all_gather | solution.py:34
  19.6 6.1 %fusion.29 = f32[16,5,2,2,32,128]{5,4,2,1,3,0:T(8,128)S(1)} fusion(bf16[16,5,2,256,128]{4,3,2,1,0:T(8,128)(2,1)} %param.6, bf16[2,32,16,256,1,1]{3,2,1,0,5,4:T(8,128)(2,1)S(1)} %bitcast_bitcast_fusion.1), kind=kOutput, calls=%fused_computation.28 | convolution fusion | flops 671088640 | bytes 16252928 | tf_op jit(solution)/shard_map/ipcnk,dsin->ipcdsk/dot_general | solution.py:24
  26.3 0.4 copy-done.1
  26.8 5.9 %fusion.55 = f32[2,2,32,5,256]{4,2,0,1,3:T(8,128)S(1)} fusion(bf16[16,5,2,256,128]{4,3,2,1,0:T(8,128)(2,1)} %param.7, f32[16,5,1,32,128]{4,3,1,0,2:T(8,128)S(1)} %fusion.48, f32[16,5,1,32,128]{4,3,1,0,2:T(8,128)S(1)} %fusion.50, f32[16,5,128]{2,1,0:T(8,128)S(1)} %fusion.74), kind=kOutput, calls=%fused_computation.57 | convolution fusion | flops 673054720 | bytes 13803520 | tf_op jit(solution)/shard_map/ipcnk,ipdsk->cdspn/dot_general | solution.py:29
  33.2 0.7 pad_maximum_fusion.2
  34.1 12.1 %psum.71 = f32[32]{0:T(128)S(1)} all-reduce(f32[32]{0:T(128)S(1)} %fusion.69), channel_id=1, replica_groups=mesh['col'=8,'row'=4] {'row'}, use_global_device_ids=true, to_apply=%region_3.0 | all-reduce | flops 32 | bytes 256 | tf_op jit(solution)/shard_map/psum | solution.py:35
  46.2 11.8 %psum.72 = f32[32]{0:T(128)S(1)} all-reduce(f32[32]{0:T(128)S(1)} %psum.71), channel_id=1, replica_groups=mesh['col'=8,'row'=4] {'col'}, use_global_device_ids=true, to_apply=%region_4.0 | all-reduce | flops 32 | bytes 256 | tf_op jit(solution)/shard_map/psum | solution.py:35
  58.0 12.7 %all-reduce.3.cloned.1.call-done = f32[2,32,1280]{2,1,0:T(8,128)} async-done(((f32[2,32,1280]{2,1,0:T(8,128)}), f32[2,32,1280]{2,1,0:T(8,128)}) %all-reduce.3.cloned.1.call-update) | async-done | bytes 327696 | tf_op jit(solution)/shard_map/psum | solution.py:36
  70.7 1.2 multiply_reduce_fusion.1
  71.9 11.8 %psum.73 = f32[32]{0:T(128)S(1)} all-reduce(f32[32]{0:T(128)S(1)} %multiply_reduce_fusion.1), channel_id=1, replica_groups=mesh['col'=8,'row'=4] {'col'}, use_global_device_ids=true, to_apply=%region_6.0 | all-reduce | flops 32 | bytes 256 | tf_op jit(solution)/shard_map/psum | solution.py:38
  83.7 1.2 fusion.78
  85.2 5.2 %fusion.20 = f32[16,5,2,2,32,128]{5,4,1,0,3,2:T(8,128)S(1)} fusion(bf16[2,32,5,256,1,1]{3,2,1,0,5,4:T(8,128)(2,1)S(1)} %bitcast.160, bf16[16,5,2,256,128]{4,3,2,1,0:T(8,128)(2,1)} %param.7), kind=kOutput, calls=%fused_computation.25 | convolution fusion | flops 671088640 | bytes 15892480 | tf_op jit(solution)/shard_map/ipcnk,dspn->ipcdsk/dot_general | solution.py:55
  90.4 1.7 fusion.47
  92.1 4.6 %fusion.32 = f32[2,2,32,16,256]{4,2,0,1,3:T(8,128)S(1)} fusion(bf16[16,5,2,256,128]{4,3,2,1,0:T(8,128)(2,1)S(1)} %bitcast.150, f32[16,5,1,32,128]{4,3,1,0,2:T(8,128)} %get-tuple-element.17, f32[16,5,1,32,128]{4,3,1,0,2:T(8,128)S(1)} %get-tuple-element.16, f32[16,5,128]{2,1,0:T(8,128)S(1)} %fusion.74), kind=kOutput, calls=%fused_computation.29 | convolution fusion | flops 673054720 | bytes 15245312 | tf_op jit(solution)/shard_map/ipcnk,ipdsk->cdsin/dot_general | solution.py:66
  96.9 0.3 copy.94
  97.3 0.3 copy.93
  97.7 1.1 pad_maximum_fusion
  98.8 34.9 %reduce-scatter.3.cloned.1.call-done = f32[2,32,512]{2,1,0:T(8,128)} async-done(((f32[2,32,4096]{2,1,0:T(8,128)}), f32[2,32,512]{2,1,0:T(8,128)}) %reduce-scatter.3.cloned.1.call-update) | async-done | bytes 131088 | tf_op jit(solution)/shard_map/reduce_scatter | solution.py:75
  133.8 1.1 multiply_reduce_fusion.3
  134.9 10.0 %all_gather.13 = bf16[2,32,4096]{2,1,0:T(8,128)(2,1)S(1)} all-gather(bf16[2,32,512]{2,1,0:T(8,128)(2,1)S(1)} %convert_element_type.38), channel_id=1, replica_groups=mesh['col'=8,'row'=4] {'col'}, dimensions={2}, use_global_device_ids=true | all-gather | bytes 589824 | tf_op jit(solution)/shard_map/all_gather | solution.py:34
  145.1 5.2 %fusion.26 = f32[16,5,2,2,32,128]{5,4,1,0,3,2:T(8,128)S(1)} fusion(bf16[2,32,16,256,1,1]{3,2,1,0,5,4:T(8,128)(2,1)S(1)} %bitcast_bitcast_fusion, bf16[16,5,2,256,128]{4,3,2,1,0:T(8,128)(2,1)} %param.6), kind=kOutput, calls=%fused_computation.27 | convolution fusion | flops 671088640 | bytes 16252928 | tf_op jit(solution)/shard_map/ipcnk,dsin->ipcdsk/dot_general | solution.py:24
  150.3 0.6 fusion.45
  151.0 0.5 slice-done.7
  151.5 0.6 slice-done.8
  152.1 3.3 %fusion.60 = f32[2,2,32,5,256]{4,2,0,1,3:T(8,128)S(1)} fusion(bf16[16,5,2,256,128]{4,3,2,1,0:T(8,128)(2,1)S(1)} %bitcast.154, f32[16,5,1,32,128]{4,3,1,0,2:T(8,128)S(1)} %get-tuple-element.15, f32[16,5,1,32,128]{4,3,1,0,2:T(8,128)S(1)} %get-tuple-element.14, f32[16,5,128]{2,1,0:T(8,128)S(1)} %fusion.74), kind=kOutput, calls=%fused_computation.58 | convolution fusion | flops 673054720 | bytes 13803520 | tf_op jit(solution)/shard_map/ipcnk,ipdsk->cdspn/dot_general | solution.py:29
  155.7 0.7 pad_maximum_fusion.3
  156.6 11.8 %psum.74 = f32[32]{0:T(128)S(1)} all-reduce(f32[32]{0:T(128)S(1)} %get-tuple-element.8), channel_id=1, replica_groups=mesh['col'=8,'row'=4] {'row'}, use_global_device_ids=true, to_apply=%region_9.0 | all-reduce | flops 32 | bytes 256 | tf_op jit(solution)/shard_map/psum | solution.py:35
  168.4 11.8 %psum.75 = f32[32]{0:T(128)S(1)} all-reduce(f32[32]{0:T(128)S(1)} %psum.74), channel_id=1, replica_groups=mesh['col'=8,'row'=4] {'col'}, use_global_device_ids=true, to_apply=%region_10.0 | all-reduce | flops 32 | bytes 256 | tf_op jit(solution)/shard_map/psum | solution.py:35
  180.2 12.9 %all-reduce.5.cloned.1.call-done = f32[2,32,1280]{2,1,0:T(8,128)} async-done(((f32[2,32,1280]{2,1,0:T(8,128)}), f32[2,32,1280]{2,1,0:T(8,128)}) %all-reduce.5.cloned.1.call-update) | async-done | bytes 327696 | tf_op jit(solution)/shard_map/psum | solution.py:36
  193.1 1.4 multiply_reduce_fusion
  194.4 11.8 %psum.77 = f32[32]{0:T(128)S(1)} all-reduce(f32[32]{0:T(128)S(1)} %multiply_reduce_fusion), channel_id=1, replica_groups=mesh['col'=8,'row'=4] {'col'}, use_global_device_ids=true, to_apply=%region_13.0 | all-reduce | flops 32 | bytes 256 | tf_op jit(solution)/shard_map/psum | solution.py:38
  206.3 1.1 fusion.76
  207.6 5.2 %fusion.23 = f32[16,5,2,2,32,128]{5,4,1,0,3,2:T(8,128)S(1)} fusion(bf16[2,32,5,256,1,1]{3,2,1,0,5,4:T(8,128)(2,1)S(1)} %bitcast.161, bf16[16,5,2,256,128]{4,3,2,1,0:T(8,128)(2,1)} %param.7), kind=kOutput, calls=%fused_computation.26 | convolution fusion | flops 671088640 | bytes 15892480 | tf_op jit(solution)/shard_map/ipcnk,dspn->ipcdsk/dot_general | solution.py:55
  212.8 1.7 fusion.43
  214.5 4.6 %fusion.35 = f32[2,2,32,16,256]{4,2,0,1,3:T(8,128)S(1)} fusion(bf16[16,5,2,256,128]{4,3,2,1,0:T(8,128)(2,1)S(1)} %bitcast.152, f32[16,5,1,32,128]{4,3,1,0,2:T(8,128)} %get-tuple-element.13, f32[16,5,1,32,128]{4,3,1,0,2:T(8,128)S(1)} %get-tuple-element.12, f32[16,5,128]{2,1,0:T(8,128)S(1)} %fusion.74), kind=kOutput, calls=%fused_computation.30 | convolution fusion | flops 673054720 | bytes 15245312 | tf_op jit(solution)/shard_map/ipcnk,ipdsk->cdsin/dot_general | solution.py:66
  219.3 0.3 copy.107
  219.7 0.3 copy.106
  220.1 1.1 pad_maximum_fusion.1
  221.6 34.7 %reduce-scatter.5.cloned.1.call-done = f32[2,32,512]{2,1,0:T(8,128)} async-done(((f32[2,32,4096]{2,1,0:T(8,128)}), f32[2,32,512]{2,1,0:T(8,128)}) %reduce-scatter.5.cloned.1.call-update) | async-done | bytes 131088 | tf_op jit(solution)/shard_map/reduce_scatter | solution.py:75
  256.2 1.1 multiply_reduce_fusion.2
  257.3 11.7 %psum.78 = f32[32]{0:T(128)S(1)} all-reduce(f32[32]{0:T(128)S(1)} %multiply_reduce_fusion.2), channel_id=1, replica_groups=mesh['col'=8,'row'=4] {'row'}, use_global_device_ids=true, to_apply=%region_16.0 | all-reduce | flops 32 | bytes 256 | tf_op jit(solution)/shard_map/psum | solution.py:35
  269.0 11.8 %psum.79 = f32[32]{0:T(128)S(1)} all-reduce(f32[32]{0:T(128)S(1)} %psum.78), channel_id=1, replica_groups=mesh['col'=8,'row'=4] {'col'}, use_global_device_ids=true, to_apply=%region_17.0 | all-reduce | flops 32 | bytes 256 | tf_op jit(solution)/shard_map/psum | solution.py:35
  280.8 0.6 divide_multiply_fusion
  281.7 10.1 %all_gather.14 = f32[2,8,10240]{2,1,0:T(8,128)S(1)} all-gather(f32[2,8,1280]{2,1,0:T(8,128)S(1)} %fusion.73), channel_id=1, replica_groups=mesh['col'=8,'row'=4] {'col'}, dimensions={2}, use_global_device_ids=true | all-gather | bytes 737280 | tf_op jit(solution)/shard_map/all_gather | solution.py:96
  291.8 0.5 gather_fusion
  292.4 14.8 %all_gather.15 = f32[2,32,1280]{2,1,0:T(8,128)S(1)} all-gather(f32[2,8,1280]{2,1,0:T(8,128)S(1)} %broadcast_select_fusion), channel_id=1, replica_groups=mesh['col'=8,'row'=4] {'row'}, dimensions={1}, use_global_device_ids=true | all-gather | bytes 409600 | tf_op jit(solution)/shard_map/all_gather | solution.py:99
  307.2 0.7 copy.221
  (78 shorter events, 3.9 us)
Async XLA Ops:
  7.2 63.5 %all-reduce.3.cloned.1.call-start = ((), (), s32[]{:S(2)}) async-start(), calls=%async_computation.2 | async-start | bytes 655360 | tf_op jit(solution)/shard_map/psum | solution.py:36
  26.0 0.7 copy-start.1
  32.7 1.3 copy-start
  33.9 99.8 %reduce-scatter.3.cloned.1.call-start = ((), (), s32[]{:S(2)}) async-start(), calls=%async_computation.3 | async-start | bytes 1179648 | tf_op jit(solution)/shard_map/reduce_scatter | solution.py:75
  83.7 8.4 %slice-start = ((s8[10485760]{0:T(1024)(128)(4,1)}), s8[2097152]{0:T(1024)(128)(4,1)S(1)}, s32[]{:S(2)}) async-start(s8[10485760]{0:T(1024)(128)(4,1)} %bitcast.149), calls=%async_computation.6 | async-start | bytes 4194304
  85.2 6.9 %slice-start.1 = ((s8[10485760]{0:T(1024)(128)(4,1)}), s8[4194304]{0:T(1024)(128)(4,1)S(1)}, s32[]{:S(2)}) async-start(s8[10485760]{0:T(1024)(128)(4,1)} %bitcast.149), calls=%async_computation.7 | async-start | bytes 8388608
  85.2 6.9 %slice-start.2 = ((s8[10485760]{0:T(1024)(128)(4,1)}), s8[4194304]{0:T(1024)(128)(4,1)S(1)}, s32[]{:S(2)}) async-start(s8[10485760]{0:T(1024)(128)(4,1)} %bitcast.149), calls=%async_computation.8 | async-start | bytes 8388608
  98.8 94.3 %all-reduce.5.cloned.1.call-start = ((), (), s32[]{:S(2)}) async-start(), calls=%async_computation.4 | async-start | bytes 655360 | tf_op jit(solution)/shard_map/psum | solution.py:36
  144.9 6.0 %slice-start.6 = ((s8[10485760]{0:T(1024)(128)(4,1)}), s8[4194304]{0:T(1024)(128)(4,1)S(1)}, s32[]{:S(2)}) async-start(s8[10485760]{0:T(1024)(128)(4,1)} %bitcast.153), calls=%async_computation.12 | async-start | bytes 8388608
  145.1 6.4 %slice-start.7 = ((s8[10485760]{0:T(1024)(128)(4,1)}), s8[4194304]{0:T(1024)(128)(4,1)S(1)}, s32[]{:S(2)}) async-start(s8[10485760]{0:T(1024)(128)(4,1)} %bitcast.153), calls=%async_computation.13 | async-start | bytes 8388608
  145.1 7.0 %slice-start.8 = ((s8[10485760]{0:T(1024)(128)(4,1)}), s8[2097152]{0:T(1024)(128)(4,1)S(1)}, s32[]{:S(2)}) async-start(s8[10485760]{0:T(1024)(128)(4,1)} %bitcast.153), calls=%async_computation.14 | async-start | bytes 4194304
  156.5 99.7 %reduce-scatter.5.cloned.1.call-start = ((), (), s32[]{:S(2)}) async-start(), calls=%async_computation.5 | async-start | bytes 1179648 | tf_op jit(solution)/shard_map/reduce_scatter | solution.py:75
  193.1 21.4 %slice-start.3 = ((s8[10485760]{0:T(1024)(128)(4,1)}), s8[2097152]{0:T(1024)(128)(4,1)S(1)}, s32[]{:S(2)}) async-start(s8[10485760]{0:T(1024)(128)(4,1)} %bitcast.151), calls=%async_computation.9 | async-start | bytes 4194304
  207.6 6.9 %slice-start.4 = ((s8[10485760]{0:T(1024)(128)(4,1)}), s8[4194304]{0:T(1024)(128)(4,1)S(1)}, s32[]{:S(2)}) async-start(s8[10485760]{0:T(1024)(128)(4,1)} %bitcast.151), calls=%async_computation.10 | async-start | bytes 8388608
  207.6 6.9 %slice-start.5 = ((s8[10485760]{0:T(1024)(128)(4,1)}), s8[4194304]{0:T(1024)(128)(4,1)S(1)}, s32[]{:S(2)}) async-start(s8[10485760]{0:T(1024)(128)(4,1)} %bitcast.151), calls=%async_computation.11 | async-start | bytes 8388608
  219.7 1.5 copy-start.2
Sparse Core Ops, SparseCore 0:
  34.0 36.5 all-reduce.2
  98.9 34.8 reduce-scatter.2
  156.6 36.4 all-reduce.4
  221.4 34.8 reduce-scatter.4
